TPU v7x, 32 devices: a whole 2x2x4 slice. The times are simulated.
32 devices in a mesh: track: 4 (over y, x), ifg: 4 (over z), pix: 2 (over core).
Axes of the slice: x: 2, y: 2, z: 4, core: 2. Of those that a mesh axis runs over, the one named last changes fastest.
Arguments:
- phases: bfloat16 [4, 600, 32768], P('track', 'ifg', 'pix')
- pairs: int32 [4, 600, 2], P('track', 'ifg'), may hold values from 0 to 249, as said below
- date_map: int32 [4, 250], replicated, may hold values from 0 to 319, as said below
- knots: int32 [32], replicated, may hold values from 0 to 319, as said below
- look: float32 [4, 3, 32768], P(None, None, 'pix'), may hold values from -1 to 1
Outputs:
- enu: float32 [3, 320, 32768], P(None, None, ('pix', 'ifg', 'track'))
- spline: float32 [3, 32, 32768], P(None, None, ('pix', 'ifg', 'track'))
Inputs may be any that keep to these rules, and one draw needn't show every extreme that they name: pairs[t, k, 0] < pairs[t, k, 1] <= pairs[t, k, 0] + 5. `date_map`: the dates of one track map to distinct epochs. `knots`: strictly increasing, the first 0 and the last 319.
All inputs are finite; a program needn't handle non-finite values.
Results may differ from a plain program's by a relative error of at most 0.0003.
Values may be sent and summed in bfloat16 or wider, within the bound.
A program may use at most 128 MiB of HBM per device.

v0:
```python
import jax
import jax.numpy as jnp
from jax import lax
from jax.sharding import PartitionSpec as P

EPOCHS = 320


damping = 0.5
ridge = 0.1
HIGH = lax.Precision.HIGHEST


def incidence(pair_rows, ndate):
    dates = jnp.arange(ndate, dtype=jnp.int32)[:, None]
    later = (dates == pair_rows[None, :, 1]).astype(jnp.float32)
    earlier = (dates == pair_rows[None, :, 0]).astype(jnp.float32)
    return later - earlier


def inverse_normal(normal_part):
    ndate = normal_part.shape[0]
    normal = normal_part + damping * jnp.eye(ndate, dtype=jnp.float32)
    factor = jnp.linalg.cholesky(normal)
    return jax.scipy.linalg.cho_solve((factor, True), jnp.eye(ndate, dtype=jnp.float32))


def hat_basis(knots, n_epochs):
    spots = knots.astype(jnp.float32)
    left = jnp.concatenate([spots[:1] - 1.0, spots[:-1]])
    right = jnp.concatenate([spots[1:], spots[-1:] + 1.0])
    epochs = jnp.arange(n_epochs, dtype=jnp.float32)[:, None]
    rise = (epochs - left) / (spots - left)
    fall = (right - epochs) / (right - spots)
    return jnp.maximum(0.0, jnp.minimum(rise, fall))


def geometry(series, date_map, look, knots, n_epochs):
    epochs = jnp.arange(n_epochs, dtype=jnp.int32)
    onehot = (date_map[:, None, :] == epochs[None, :, None]).astype(jnp.float32)
    seen = jnp.sum(onehot, axis=2)
    resampled = jnp.einsum("tcd,tdp->tcp", onehot, series, precision=HIGH)

    def entry(first, second):
        value = jnp.einsum("tc,tp->cp", seen, look[:, first] * look[:, second], precision=HIGH)
        if first == second:
            value = value + ridge
        return value

    a00, a01, a02 = (entry(0, 0), entry(0, 1), entry(0, 2))
    a11, a12, a22 = (entry(1, 1), entry(1, 2), entry(2, 2))
    b_all = [jnp.sum(look[:, i][:, None, :] * resampled, axis=0) for i in range(3)]
    c00 = a11 * a22 - a12 * a12
    c01 = a02 * a12 - a01 * a22
    c02 = a01 * a12 - a02 * a11
    c11 = a00 * a22 - a02 * a02
    c12 = a01 * a02 - a00 * a12
    c22 = a00 * a11 - a01 * a01
    det = a00 * c00 + a01 * c01 + a02 * c02
    east = (c00 * b_all[0] + c01 * b_all[1] + c02 * b_all[2]) / det
    north = (c01 * b_all[0] + c11 * b_all[1] + c12 * b_all[2]) / det
    upward = (c02 * b_all[0] + c12 * b_all[1] + c22 * b_all[2]) / det
    enu = jnp.stack([east, north, upward])
    basis = hat_basis(knots, n_epochs)
    gram = jnp.dot(basis.T, basis, precision=HIGH)
    factor = jnp.linalg.cholesky(gram)
    fitter = jax.scipy.linalg.cho_solve((factor, True), basis.T)
    spline = jnp.einsum("kc,icp->ikp", fitter, enu, precision=HIGH)
    return (enu, spline)


def shards(phases, pairs, date_map, knots, look):
    ndate = date_map.shape[1]
    n_epochs = hat_count()
    n_track = lax.axis_size("track")
    n_ifg = lax.axis_size("ifg")
    width = phases.shape[2] // (n_track * n_ifg)
    offset = lax.axis_index("ifg") * (width * n_track) + lax.axis_index("track") * width
    look_local = lax.dynamic_slice_in_dim(look, offset, width, 2)
    phase_rows = phases[0]
    pair_rows = pairs[0]
    phase_all = lax.all_to_all(phase_rows, "ifg", split_axis=1, concat_axis=0, tiled=True)
    pair_all = lax.all_gather(pair_rows, "ifg", axis=0, tiled=True)
    incid = incidence(pair_all, ndate)
    normal_part = jnp.dot(incid, incid.T, precision=HIGH)
    rhs = jnp.dot(incid.astype(jnp.bfloat16), phase_all, preferred_element_type=jnp.float32)
    ninv = inverse_normal(normal_part)
    pixel_count = rhs.shape[1] * lax.axis_size("ifg") * lax.axis_size("pix")
    series = jnp.dot(ninv, rhs, precision=HIGH)
    total = lax.psum(jnp.sum(series, axis=1), ("ifg", "pix"))
    series = series - (total / pixel_count)[:, None]
    gathered = lax.all_to_all(series[None], "track", split_axis=2, concat_axis=0, tiled=True)
    return geometry(gathered, date_map, look_local, knots, n_epochs)


def hat_count():
    return EPOCHS


def solution(mesh):
    in_specs = (P("track", "ifg", "pix"), P("track", "ifg", None), P(), P(), P(None, None, "pix"))
    out_specs = (P(None, None, ("pix", "ifg", "track")), P(None, None, ("pix", "ifg", "track")))
    return jax.shard_map(shards, mesh=mesh, in_specs=in_specs, out_specs=out_specs, check_vma=False)
```

profile of v0, /device:TPU:0, one launch (start us, length us, event | category | flops | bytes accessed | tf_op | source)
XLA Modules:
  0.0 324.2 jit_solution(3422282366233087118)
XLA Ops:
  0.6 11.1 %all_to_all.27 = bf16[150,4,4096]{2,1,0:T(4,128)(2,1)} reshape(bf16[1,150,16384]{2,1,0:T(8,128)(2,1)} %param.5) | data formatting | bytes 9830400 | tf_op jit(solution)/shard_map/all_to_all | solution.py:82
  11.7 7.3 %copy.23 = bf16[150,4,4096]{2,0,1:T(8,128)(2,1)} copy(bf16[150,4,4096]{2,1,0:T(4,128)(2,1)} %all_to_all.27) | data formatting | bytes 9830400 | tf_op jit(solution)/shard_map/all_to_all | solution.py:82
  19.1 6.5 %all-to-all-start = ((bf16[150,4,4096]{2,0,1:T(8,128)(2,1)}), bf16[150,4,4096]{2,0,1:T(8,128)(2,1)}, u32[]{:S(2)}, u32[]{:S(2)}) async-start(bf16[150,4,4096]{2,0,1:T(8,128)(2,1)} %copy.23), calls=%async_computation | async-start | bytes 9961472 | tf_op jit(solution)/shard_map/all_to_all | solution.py:82
  25.6 0.0 copy-done.5
  25.6 0.1 copy.21
  25.7 118.2 %all-gather = s32[1,600,2]{2,0,1:T(1,128)S(1)} all-gather(s32[1,150,2]{2,0,1:T(1,128)S(1)} %copy.21), channel_id=2, replica_groups=mesh['track'=4,'ifg'=4,'pix'=2] {'ifg'}, dimensions={1}, use_global_device_ids=true | all-gather | bytes 6000 | tf_op jit(solution)/shard_map/all_gather | solution.py:83
  143.9 0.3 slice_reduce_fusion.1
  144.3 1.0 fusion.3
  145.3 0.1 copy.22
  145.5 0.1 fusion.16
  145.5 0.0 copy-start.6
  145.5 11.7 %cholesky.63 = f32[128,128]{1,0:T(8,128)S(1)} custom-call(f32[128,128]{1,0:T(8,128)S(1)} %cholesky.156), custom_call_target="Cholesky" | custom-call | tf_op jit(solution)/shard_map/jit(cholesky)/cholesky | solution.py:24
  157.3 9.8 %custom-call.28 = f32[1,128,128]{1,2,0:T(8,128)S(1)} custom-call(f32[1,128,128]{2,1,0:T(8,128)S(1)} %get-tuple-element.40), custom_call_target="InvertDiagBlocksLowerTriangular" | custom-call | tf_op jit(solution)/shard_map/jit(cholesky)/cholesky | solution.py:24
  167.1 0.2 constant_dynamic-update-slice_fusion
  167.3 0.3 convolution_subtract_fusion.2
  167.6 11.2 %cholesky.133 = f32[122,122]{1,0:T(8,128)S(1)} custom-call(f32[122,122]{1,0:T(8,128)S(1)} %convolution_subtract_fusion.2), custom_call_target="Cholesky" | custom-call | tf_op jit(solution)/shard_map/jit(cholesky)/cholesky | solution.py:24
  178.8 0.6 compare_reduce_fusion.1
  179.5 0.6 compare_reduce_fusion.2
  181.5 0.1 fusion.21
  181.6 19.8 %custom-call.29 = f32[2,128,128]{1,2,0:T(8,128)S(1)} custom-call(f32[2,128,128]{2,1,0:T(8,128)S(1)} %pad_maximum_fusion.1), custom_call_target="InvertDiagBlocksLowerTriangular" | custom-call | tf_op jit(solution)/shard_map/jit(_cho_solve)/triangular_solve | solution.py:25
  201.5 0.1 fusion.47
  201.6 0.3 fusion.17
  201.8 0.3 convolution_subtract_fusion.1
  202.1 0.3 fusion.27
  202.4 0.3 fusion.26
  202.7 0.3 convolution_subtract_fusion
  203.0 0.3 fusion.25
  203.3 0.0 all-to-all-done
  203.3 6.0 %all_to_all.30 = bf16[600,4096]{1,0:T(8,128)(2,1)} reshape(bf16[4,150,4096]{2,1,0:T(8,128)(2,1)} %bitcast.11) | data formatting | bytes 9830400 | tf_op jit(solution)/shard_map/all_to_all | solution.py:82
  209.2 4.2 %fusion.5 = f32[250,4096]{1,0:T(8,128)S(1)} fusion(bf16[600,4096]{1,0:T(8,128)(2,1)} %all_to_all.30, s32[600]{0:T(1024)S(1)} %get-tuple-element.26, s32[600]{0:T(1024)S(1)} %get-tuple-element.25), kind=kOutput, calls=%fused_computation.31 | convolution fusion | flops 1229699968 | bytes 9016000 | tf_op jit(solution)/shard_map/dot_general | solution.py:86
  213.5 5.3 %fusion.48 = (f32[250]{0:T(256)S(1)}, f32[250,4096]{1,0:T(8,128)}) fusion(f32[250,4096]{1,0:T(8,128)S(1)} %fusion.5, f32[122,250]{1,0:T(8,128)S(1)} %fusion.26, f32[128,250]{1,0:T(8,128)S(1)} %fusion.25), kind=kOutput, calls=%fused_computation.113 | convolution fusion | flops 3073086208 | bytes 8443000 | tf_op jit(solution)/shard_map/dot_general | solution.py:89
  218.8 13.6 %psum.7 = f32[250]{0:T(256)S(1)} all-reduce(f32[250]{0:T(256)S(1)} %get-tuple-element.49), channel_id=1, replica_groups=mesh['track'=4,'ifg'=4,'pix'=2] {'ifg','pix'}, use_global_device_ids=true, to_apply=%region_6.7 | all-reduce | flops 250 | bytes 2000 | tf_op jit(solution)/shard_map/psum | solution.py:90
  232.3 4.7 %subtract_bitcast_fusion = f32[1,250,4096]{2,1,0:T(8,128)} fusion(f32[250,4096]{1,0:T(8,128)} %get-tuple-element.50, f32[250]{0:T(256)S(1)} %broadcast_multiply_fusion), kind=kLoop, calls=%fused_computation.5 | loop fusion | flops 1024000 | bytes 8193000 | tf_op jit(solution)/shard_map/broadcast_in_dim | solution.py:92
  237.0 10.2 %copy.24 = f32[1,250,4096]{1,0,2:T(1,128)} copy(f32[1,250,4096]{2,1,0:T(8,128)} %subtract_bitcast_fusion) | data formatting | bytes 8192000 | tf_op jit(solution)/shard_map/broadcast_in_dim | solution.py:92
  247.2 5.1 %all-to-all-start.1 = ((f32[1,250,4096]{1,0,2:T(1,128)}), f32[1,250,4096]{1,0,2:T(1,128)}, u32[]{:S(2)}, u32[]{:S(2)}) async-start(f32[1,250,4096]{1,0,2:T(1,128)} %copy.24), calls=%async_computation.1 | async-start | bytes 8388608 | tf_op jit(solution)/shard_map/all_to_all | solution.py:92
  252.3 0.6 fusion.46
  254.2 0.1 convert_subtract_fusion.3
  254.3 0.4 fusion.20
  254.7 0.1 copy.26
  254.8 2.9 cholesky.147
  257.8 0.6 compare_reduce_fusion
  258.4 0.7 fusion.30
  259.1 2.4 custom-call.30
  261.5 0.8 dynamic-slice_bitcast_fusion.2
  262.3 0.3 fusion.19
  262.7 0.2 convolution_bitcast_fusion.1
  262.9 0.3 convert_reduce_fusion
  263.1 2.4 convolution_add_fusion
  265.5 2.4 convolution_add_fusion.1
  267.9 2.3 convolution_add_fusion.2
  270.2 1.2 fusion.35
  271.5 1.3 fusion.37
  272.7 27.3 %all-to-all-done.1 = f32[1,250,4096]{1,0,2:T(1,128)} async-done(((f32[1,250,4096]{1,0,2:T(1,128)}), f32[1,250,4096]{1,0,2:T(1,128)}, u32[]{:S(2)}, u32[]{:S(2)}) %all-to-all-start.1) | async-done | bytes 4096032 | tf_op jit(solution)/shard_map/all_to_all | solution.py:92
  300.0 4.4 %copy.27 = f32[1,250,4096]{1,2,0:T(8,128)} copy(f32[1,250,4096]{1,0,2:T(1,128)} %all-to-all-done.1) | data formatting | bytes 8192000
  304.4 5.6 %copy.25 = f32[1,250,4,1024]{3,1,2,0:T(8,128)} copy(f32[1,250,4,1024]{1,3,2,0:T(8,128)} %bitcast.82) | data formatting | bytes 8192000 | tf_op jit(solution)/shard_map/all_to_all | solution.py:92
  310.1 0.0 copy-start.1
  310.1 0.0 copy-start.2
  310.1 0.0 copy-start.3
  310.1 6.9 %multiply_reduce_fusion.2 = (f32[320,1024]{1,0:T(8,128)S(1)}, f32[320,1024]{1,0:T(8,128)S(1)}, f32[320,1024]{1,0:T(8,128)S(1)}) fusion(f32[4,1024]{1,0:T(4,128)S(1)} %get-tuple-element.36, f32[4,1024]{1,0:T(4,128)S(1)} %get-tuple-element.35, f32[4,1024]{1,0:T(4,128)S(1)} %get-tuple-element.34, f32[1,250,4,1024]{3,1,2,0:T(8,128)} %copy.25, ...), kind=kOutput, calls=%fused_computation.2 | convolution fusion | flops 3939361280 | bytes 8081312 | tf_op jit(solution)/shard_map/tcd,tdp->tcp/dot_general | solution.py:42
  317.1 3.0 divide_bitcast_fusion.2
  320.1 0.5 pad_maximum_fusion
  320.6 0.0 copy-start
  320.6 3.3 %convolution_bitcast_fusion = f32[3,32,1024]{2,1,0:T(8,128)} fusion(f32[3,320,1024]{2,1,0:T(8,128)S(1)} %pad_maximum_fusion, f32[32,320,1]{1,0,2:T(8,128)S(1)} %convolution_bitcast_fusion.1), kind=kOutput, calls=%fused_computation.20 | convolution fusion | flops 377487360 | bytes 4366336 | tf_op jit(solution)/shard_map/kc,icp->ikp/dot_general | solution.py:68
  323.9 0.0 copy-done
  (21 shorter events, 0.3 us)
Async XLA Ops:
  19.1 6.5 %copy-start.5 = (s32[1,150,2]{1,2,0:T(2,128)S(1)}, s32[1,150,2]{1,2,0:T(2,128)}, u32[]{:S(2)}) copy-start(s32[1,150,2]{1,2,0:T(2,128)} %param.6) | copy-start | bytes 3604
  19.1 184.2 %all-to-all-start = ((bf16[150,4,4096]{2,0,1:T(8,128)(2,1)}), bf16[150,4,4096]{2,0,1:T(8,128)(2,1)}, u32[]{:S(2)}, u32[]{:S(2)}) async-start(bf16[150,4,4096]{2,0,1:T(8,128)(2,1)} %copy.23), calls=%async_computation | async-start | bytes 9961472 | tf_op jit(solution)/shard_map/all_to_all | solution.py:82
  145.5 55.9 %copy-start.6 = (s32[32]{0:T(128)S(1)}, s32[32]{0:T(128)}, u32[]{:S(2)}) copy-start(s32[32]{0:T(128)} %param.8) | copy-start | bytes 388
  247.2 52.8 %all-to-all-start.1 = ((f32[1,250,4096]{1,0,2:T(1,128)}), f32[1,250,4096]{1,0,2:T(1,128)}, u32[]{:S(2)}, u32[]{:S(2)}) async-start(f32[1,250,4096]{1,0,2:T(1,128)} %copy.24), calls=%async_computation.1 | async-start | bytes 8388608 | tf_op jit(solution)/shard_map/all_to_all | solution.py:92
  254.3 8.6 %copy-start.4 = (s32[4,250]{1,0:T(4,128)S(1)}, s32[4,250]{1,0:T(4,128)}, u32[]{:S(2)}) copy-start(s32[4,250]{1,0:T(4,128)} %param.7) | copy-start | bytes 12004
  310.1 6.9 %copy-start.1 = (f32[320,1024]{1,0:T(8,128)S(1)}, f32[320,1024]{1,0:T(8,128)}, u32[]{:S(2)}) copy-start(f32[320,1024]{1,0:T(8,128)} %convolution_add_fusion) | copy-start | bytes 3932164
  310.1 6.9 %copy-start.2 = (f32[320,1024]{1,0:T(8,128)S(1)}, f32[320,1024]{1,0:T(8,128)}, u32[]{:S(2)}) copy-start(f32[320,1024]{1,0:T(8,128)} %convolution_add_fusion.1) | copy-start | bytes 3932164
  310.1 6.9 %copy-start.3 = (f32[320,1024]{1,0:T(8,128)S(1)}, f32[320,1024]{1,0:T(8,128)}, u32[]{:S(2)}) copy-start(f32[320,1024]{1,0:T(8,128)} %convolution_add_fusion.2) | copy-start | bytes 3932164
  320.6 3.3 %copy-start = (f32[3,320,1024]{2,1,0:T(8,128)}, f32[3,320,1024]{2,1,0:T(8,128)S(1)}, u32[]{:S(2)}) copy-start(f32[3,320,1024]{2,1,0:T(8,128)S(1)} %pad_maximum_fusion) | copy-start | bytes 11796484
where the time goes:
time: 329 us; the launch traced here: 324 us
  blocking collectives  132 us (40%)
  other arithmetic  66.4 us (20%)
  local copies, waits for them, and re-layouts  46.8 us (14%)
  matrix products  36.4 us (11%)
  waiting for transfers between devices  27.3 us (8%)
  starting transfers between devices  11.5 us (3%)
  between operations  3.88 us (1%)
    all_gather x1, blocking collectives, shards(): pair_all = lax.all_gather(pair_rows, 'ifg', axis=0, tiled=True)  118 us
    another operation x7, other arithmetic, inverse_normal(): factor = jnp.linalg.cholesky(normal)  34 us
    all_to_all x1, waiting for transfers between devices, shards(): lax.all_to_all(series[None], 'track', split_axis=2, concat_axis=0, tiled=...  27.3 us
    all_to_all x3, local copies, waits for them, and re-layouts, shards(): lax.all_to_all(phase_rows, 'ifg', split_axis=1, concat_axis=0, tiled=True)  24.4 us
    another operation x6, other arithmetic, inverse_normal(): jax.scipy.linalg.cho_solve((factor, True), jnp.eye(ndate, dtype=jnp.float...  20 us
    psum x1, blocking collectives, shards(): total = lax.psum(jnp.sum(series, axis=1), ('ifg', 'pix'))  13.6 us
    dot_general x6, matrix products, entry(): jnp.einsum('tc,tp->cp', seen, look[:, first] * look[:, second], precision...  12.6 us
    broadcast_in_dim x1, local copies, waits for them, and re-layouts, shards(): series[None]  10.2 us
  transfers between devices with their start and end apart: 2, of which 1 were waited for; matrix products, arithmetic and copies ran while one was open for 24% of the time, Pallas kernels for 0%

commit v1 on v0

v1 whole, which is shorter than its diff:
```python
import functools
import math

import jax
import jax.numpy as jnp
from jax import lax
from jax.experimental import pallas as pl
from jax.experimental.pallas import tpu as pltpu
from jax.sharding import PartitionSpec as P

EPOCHS = 320
DAMPING = 0.5
RIDGE = 0.1
HIGH = lax.Precision.HIGHEST
MESH = pl.DeviceIdType.MESH
NT = (((1,), (1,)), ((), ()))


def dot(a, b):
    return jnp.dot(a, b, precision=HIGH, preferred_element_type=jnp.float32)


def partner(index, step, count):
    if count & (count - 1) == 0:
        return lax.bitwise_xor(index, step)
    return lax.rem(index + step, count)


def exchange_kernel(n_track, n_ifg, n_pix, pixels, ndate, ph, pairs, dmap, spots, out, r_out, meta, fitter,
                    pairs_all, normal, inverse, r_full, local, sums_pix, sums_all,
                    send, recv, p_send, p_recv, x_send, x_recv, s_send, s_recv, l_sem):
    t, i, x = lax.axis_index("track"), lax.axis_index("ifg"), lax.axis_index("pix")
    width = out.shape[-1]
    ifgs = ph.shape[0]
    epochs = fitter.shape[1]
    order = sorted(range(n_ifg), key=lambda s: (s == 0, -(s >= n_ifg // 2), s))
    steps = [(dt, di) for di in order for dt in reversed(range(n_track)) if (dt, di) != (0, 0)]

    def peer(dt, di):
        return {"track": partner(t, dt, n_track), "ifg": partner(i, di, n_ifg)}

    bar = pltpu.get_barrier_semaphore()
    for dt, di in steps:
        pl.semaphore_signal(bar, inc=1, device_id=peer(dt, di), device_id_type=MESH)
    for dx in range(1, n_pix):
        pl.semaphore_signal(bar, inc=1, device_id={"pix": partner(x, dx, n_pix)}, device_id_type=MESH)
    pl.semaphore_wait(bar, len(steps) + n_pix - 1)

    def remote(src, dst, ssem, rsem, device):
        return pltpu.make_async_remote_copy(src_ref=src, dst_ref=dst, send_sem=ssem, recv_sem=rsem,
                                            device_id=device, device_id_type=MESH)

    pair_copies, phase_copies = [], []
    for dt, di in steps:
        at = dt * n_ifg + di
        copy = remote(pairs, pairs_all.at[t, i], p_send.at[at], p_recv.at[at], peer(dt, di))
        copy.start()
        pair_copies.append(copy)

    def send_phases(dt, di):
        at = dt * n_ifg + di
        where = peer(dt, di)
        column = pl.multiple_of((where["ifg"] * n_track + where["track"]) * width, width)
        copy = remote(ph.at[:, pl.ds(column, width)], out.at[t, i], send.at[at], recv.at[at], where)
        copy.start()
        phase_copies.append(copy)

    early = [s for s in steps if s[1] >= max(1, n_ifg // 2)]
    late = [s for s in steps if s not in early]
    for s in early:
        send_phases(*s)
    load = pltpu.make_async_copy(ph, local, l_sem.at[0])
    load.start()
    own_pairs = pltpu.make_async_copy(pairs, pairs_all.at[t, i], l_sem.at[1])
    own_pairs.start()
    column = pl.multiple_of((i * n_track + t) * width, width)
    own = pltpu.make_async_copy(ph.at[:, pl.ds(column, width)], out.at[t, i], l_sem.at[2])
    own.start()

    load.wait()
    ones = jnp.ones((8, width), jnp.bfloat16)

    def add_columns(step, total):
        part = local[:, pl.ds(pl.multiple_of(step * width, width), width)]
        return total + lax.dot_general(ones, part, NT, preferred_element_type=jnp.float32)

    row_sums = lax.fori_loop(0, ph.shape[1] // width, add_columns, jnp.zeros((8, ifgs), jnp.float32))
    sums_pix[x] = row_sums

    own_pairs.wait()
    for copy in pair_copies:
        copy.wait()

    def incidence(track, piece):
        dates = lax.broadcasted_iota(jnp.int32, (ndate, ifgs), 0)
        first = pairs_all[track, piece, 0:1, :]
        second = pairs_all[track, piece, 1:2, :]
        return (dates == second).astype(jnp.float32) - (dates == first).astype(jnp.float32)

    def eye(n):
        return (lax.broadcasted_iota(jnp.int32, (n, n), 0) == lax.broadcasted_iota(jnp.int32, (n, n), 1)).astype(jnp.float32)

    total_ifgs = ifgs * n_ifg
    scale = 2.0 / (2.0 * DAMPING + 2.0 * total_ifgs)
    for track in range(n_track):
        value = DAMPING * eye(ndate)
        for piece in range(n_ifg):
            part = incidence(track, piece).astype(jnp.bfloat16)
            value = value + lax.dot_general(part, part, NT, preferred_element_type=jnp.float32)
        normal[track] = value
        inverse[track] = scale * eye(ndate)

    pix_copies = []
    for dx in range(1, n_pix):
        copy = remote(sums_pix.at[x], sums_pix.at[x], x_send.at[dx], x_recv.at[dx], {"pix": partner(x, dx, n_pix)})
        copy.start()
        pix_copies.append(copy)
    for copy in pix_copies:
        copy.wait()
    gathered = sums_pix[0]
    for k in range(1, n_pix):
        gathered = gathered + sums_pix[k]
    sums_all[t, i] = gathered

    spot, left, right = spots[0:1, :], spots[1:2, :], spots[2:3, :]
    knots = spots.shape[1]
    epoch = lax.broadcasted_iota(jnp.int32, (epochs, knots), 0).astype(jnp.float32)
    basis = jnp.maximum(0.0, jnp.minimum((epoch - left) / (spot - left), (right - epoch) / (right - spot)))
    gram = lax.dot_general(basis, basis, (((0,), (0,)), ((), ())), precision=HIGH, preferred_element_type=jnp.float32)
    unit = eye(knots)
    guess = unit / jnp.sum(gram * unit, axis=1, keepdims=True)
    for _ in range(6):
        guess = 2.0 * guess - dot(guess, dot(gram, guess))
    fitter[...] = lax.dot_general(guess, basis, NT, precision=HIGH, preferred_element_type=jnp.float32)

    sum_copies = []
    for dt, di in steps:
        at = dt * n_ifg + di
        copy = remote(sums_all.at[t, i], sums_all.at[t, i], s_send.at[at], s_recv.at[at], peer(dt, di))
        copy.start()
        sum_copies.append(copy)
    for s in late:
        send_phases(*s)

    rounds = math.ceil(math.log2(18.0 * (1.0 + 2.0 * total_ifgs / (2.0 * DAMPING)))) + 1

    def newton(_, carry):
        for track in range(n_track):
            now = inverse[track]
            inverse[track] = 2.0 * now - dot(now, dot(normal[track], now))
        return carry

    lax.fori_loop(0, rounds, newton, 0)

    for track in range(n_track):
        hot = (lax.broadcasted_iota(jnp.int32, (epochs, ndate), 0) == dmap[track:track + 1, :]).astype(jnp.float32)
        rows = dot(hot, inverse[track])
        for piece in range(n_ifg):
            full = dot(rows, incidence(track, piece))
            r_full[track, piece] = full
            high = full.astype(jnp.bfloat16)
            r_out[track, piece, :epochs, :] = high
            r_out[track, piece, epochs:, :] = (full - high.astype(jnp.float32)).astype(jnp.bfloat16)

    for copy in sum_copies:
        copy.wait()
    for track in range(n_track):
        hot = (lax.broadcasted_iota(jnp.int32, (epochs, ndate), 0) == dmap[track:track + 1, :]).astype(jnp.float32)
        seen = jnp.sum(hot, axis=1, keepdims=True)
        mean = jnp.zeros((epochs, 1), jnp.float32)
        for piece in range(n_ifg):
            mean = mean + jnp.sum(r_full[track, piece] * sums_all[track, piece, 0:1, :], axis=1, keepdims=True)
        lane = lax.broadcasted_iota(jnp.int32, (epochs, 128), 1)
        meta[track] = jnp.where(lane == 0, mean * (1.0 / pixels), seen)
    own.wait()
    for copy in phase_copies:
        copy.wait()


def geometry_kernel(ph, r, meta, fitter, look, enu, spline):
    n_track, n_ifg = ph.shape[:2]
    epochs = enu.shape[1]
    terms = []
    for track in range(n_track):
        both = jnp.dot(r[track, 0], ph[track, 0], preferred_element_type=jnp.float32)
        for piece in range(1, n_ifg):
            both = both + jnp.dot(r[track, piece], ph[track, piece], preferred_element_type=jnp.float32)
        terms.append(both[:epochs] + both[epochs:] - meta[track, :, 0:1])
    seen = [meta[track, :, 1:2] for track in range(n_track)]
    rows = [[look[track, j:j + 1, :] for j in range(3)] for track in range(n_track)]

    def entry(a, b):
        value = RIDGE if a == b else 0.0
        for track in range(n_track):
            value = value + seen[track] * (rows[track][a] * rows[track][b])
        return value

    a00, a01, a02 = entry(0, 0), entry(0, 1), entry(0, 2)
    a11, a12, a22 = entry(1, 1), entry(1, 2), entry(2, 2)
    b = []
    for j in range(3):
        value = rows[0][j] * terms[0]
        for track in range(1, n_track):
            value = value + rows[track][j] * terms[track]
        b.append(value)
    c00 = a11 * a22 - a12 * a12
    c01 = a02 * a12 - a01 * a22
    c02 = a01 * a12 - a02 * a11
    c11 = a00 * a22 - a02 * a02
    c12 = a01 * a02 - a00 * a12
    c22 = a00 * a11 - a01 * a01
    inv = 1.0 / (a00 * c00 + a01 * c01 + a02 * c02)
    enu[0] = (c00 * b[0] + c01 * b[1] + c02 * b[2]) * inv
    enu[1] = (c01 * b[0] + c11 * b[1] + c12 * b[2]) * inv
    enu[2] = (c02 * b[0] + c12 * b[1] + c22 * b[2]) * inv
    for j in range(3):
        spline[j] = dot(fitter[...], enu[j])


def shards(sizes, phases, pairs, date_map, knots, look):
    n_track, n_ifg, n_pix = sizes
    ifgs, columns = phases.shape[1:]
    width = columns // (n_track * n_ifg)
    ndate, n_knots = date_map.shape[1], knots.shape[0]
    peers = n_track * n_ifg
    spots = knots.astype(jnp.float32)
    spots = jnp.stack([spots, jnp.concatenate([spots[:1] - 1.0, spots[:-1]]),
                       jnp.concatenate([spots[1:], spots[-1:] + 1.0])])
    vmem = pl.BlockSpec(memory_space=pltpu.VMEM)
    anywhere = pl.BlockSpec(memory_space=pl.ANY)
    dma = lambda n: pltpu.SemaphoreType.DMA((n,))
    gathered, r, meta, fitter = pl.pallas_call(
        functools.partial(exchange_kernel, n_track, n_ifg, n_pix, columns * n_pix, ndate),
        out_shape=(
            jax.ShapeDtypeStruct((n_track, n_ifg, ifgs, width), phases.dtype),
            jax.ShapeDtypeStruct((n_track, n_ifg, 2 * EPOCHS, ifgs), jnp.bfloat16),
            jax.ShapeDtypeStruct((n_track, EPOCHS, 128), jnp.float32),
            jax.ShapeDtypeStruct((n_knots, EPOCHS), jnp.float32),
        ),
        in_specs=[anywhere, vmem, vmem, vmem],
        out_specs=(anywhere, vmem, vmem, vmem),
        scratch_shapes=[
            pltpu.VMEM((n_track, n_ifg, 2, ifgs), jnp.int32),
            pltpu.VMEM((n_track, ndate, ndate), jnp.float32),
            pltpu.VMEM((n_track, ndate, ndate), jnp.float32),
            pltpu.VMEM((n_track, n_ifg, EPOCHS, ifgs), jnp.float32),
            pltpu.VMEM((ifgs, columns), phases.dtype),
            pltpu.VMEM((n_pix, 8, ifgs), jnp.float32),
            pltpu.VMEM((n_track, n_ifg, 8, ifgs), jnp.float32),
            dma(peers), dma(peers), dma(peers), dma(peers), dma(n_pix), dma(n_pix), dma(peers), dma(peers), dma(3),
        ],
        compiler_params=pltpu.CompilerParams(collective_id=0, has_side_effects=True, vmem_limit_bytes=48 << 20),
        name="exchange",
    )(phases[0], pairs[0].T, date_map, spots)

    offset = (lax.axis_index("ifg") * n_track + lax.axis_index("track")) * width
    look_local = lax.dynamic_slice_in_dim(look, offset, width, 2)
    block = min(256, width)
    return tuple(pl.pallas_call(
        geometry_kernel,
        grid=(width // block,),
        out_shape=(
            jax.ShapeDtypeStruct((3, EPOCHS, width), jnp.float32),
            jax.ShapeDtypeStruct((3, n_knots, width), jnp.float32),
        ),
        in_specs=[
            pl.BlockSpec((n_track, n_ifg, ifgs, block), lambda g: (0, 0, 0, g)),
            pl.BlockSpec((n_track, n_ifg, 2 * EPOCHS, ifgs), lambda g: (0, 0, 0, 0)),
            pl.BlockSpec((n_track, EPOCHS, 128), lambda g: (0, 0, 0)),
            pl.BlockSpec((n_knots, EPOCHS), lambda g: (0, 0)),
            pl.BlockSpec((n_track, 3, block), lambda g: (0, 0, g)),
        ],
        out_specs=(
            pl.BlockSpec((3, EPOCHS, block), lambda g: (0, 0, g)),
            pl.BlockSpec((3, n_knots, block), lambda g: (0, 0, g)),
        ),
        compiler_params=pltpu.CompilerParams(vmem_limit_bytes=60 << 20),
        name="geometry",
    )(gathered, r, meta, fitter, look_local))


def solution(mesh):
    sizes = tuple(mesh.shape[name] for name in ("track", "ifg", "pix"))
    in_specs = (P("track", "ifg", "pix"), P("track", "ifg", None), P(), P(), P(None, None, "pix"))
    out_specs = (P(None, None, ("pix", "ifg", "track")), P(None, None, ("pix", "ifg", "track")))
    return jax.shard_map(functools.partial(shards, sizes), mesh=mesh, in_specs=in_specs, out_specs=out_specs, check_vma=False)
```

time: 329 us -> 156 us (0.47); the launches traced: 324 us -> 156 us
  Pallas kernels: 0 us -> 147 us
  blocking collectives: 132 us -> 0 us
  other arithmetic: 66.4 us -> 0.82 us
  local copies, waits for them, and re-layouts: 46.8 us -> 6.44 us
  matrix products: 36.4 us -> 0 us
  waiting for transfers between devices: 27.3 us -> 0 us
  starting transfers between devices: 11.5 us -> 0 us
    pallas_call x0 -> x2, Pallas kernels: none -> 147 us  [the longest x1 131 us: shards(): pl.pallas_call(functools.partial(exchange_kernel, n_track, n_ifg, n_pix,...]
    all_gather x1 -> x0, blocking collectives: 118 us -> none  [shards(): pair_all = lax.all_gather(pair_rows, 'ifg', axis=0, tiled=True)]
    another operation x19 -> x3, other arithmetic: 61.2 us -> 0.82 us  [shards(): jnp.stack([spots, jnp.concatenate([spots[:1] - 1.0, spots[:-1]]), jnp.con...]
    dot_general x12 -> x0, matrix products: 33.8 us -> none  [the longest x6 12.6 us: entry(): jnp.einsum('tc,tp->cp', seen, look[:, first] * look[:, second], precision...]
    all_to_all x4 -> x0, local copies, waits for them, and re-layouts: 30 us -> none  [the longest x3 24.4 us: shards(): lax.all_to_all(phase_rows, 'ifg', split_axis=1, concat_axis=0, tiled=True)]
    all_to_all x2 -> x0, waiting for transfers between devices: 27.3 us -> none  [the longest x1 27.3 us: shards(): lax.all_to_all(series[None], 'track', split_axis=2, concat_axis=0, tiled=...]
    psum x1 -> x0, blocking collectives: 13.6 us -> none  [shards(): total = lax.psum(jnp.sum(series, axis=1), ('ifg', 'pix'))]
    all_to_all x2 -> x0, starting transfers between devices: 11.5 us -> none  [the longest x1 6.48 us: shards(): lax.all_to_all(phase_rows, 'ifg', split_axis=1, concat_axis=0, tiled=True)]
  transfers between devices with their start and end apart: 2 -> 0, of which waited for: 1 -> 0; matrix products, arithmetic and copies ran while one was open for 24% -> 0% of each run, Pallas kernels for 0% -> 0%
where the time goes in v1:
time: 156 us
  Pallas kernels  147 us (94%)
  local copies, waits for them, and re-layouts  6.44 us (4%)
  between operations  1.98 us (1%)
    pallas_call x1, Pallas kernels, shards(): pl.pallas_call(functools.partial(exchange_kernel, n_track, n_ifg, n_pix,...  131 us
    pallas_call x1, Pallas kernels, shards(): pl.pallas_call(geometry_kernel, grid=(width // block,), out_shape=(jax.Sh...  16.1 us
    unnamed x13, local copies, waits for them, and re-layouts  5.77 us

profile of v1, /device:TPU:0, one launch (start us, length us, event | category | flops | bytes accessed | tf_op | source)
XLA Modules:
  0.0 156.0 jit_solution(12190270439598456156)
XLA Ops:
  0.6 0.0 copy-start
  0.7 0.7 convert_bitcast_fusion
  1.4 0.6 fusion
  3.3 0.1 fusion.1
  3.3 0.1 maximum_bitcast_fusion
  3.4 0.0 copy-done
  3.5 0.7 copy.8.look
  4.1 0.0 copy-start.4
  4.1 0.7 copy-done.4
  4.8 0.0 copy-start.5
  4.8 0.7 copy-done.5
  5.5 130.7 %exchange.1 = (bf16[4,4,150,1024]{3,2,1,0:T(8,128)(2,1)S(1)}, bf16[4,4,640,150]{3,2,1,0:T(8,128)(2,1)}, f32[4,320,128]{2,1,0:T(8,128)S(1)}, f32[32,320]{1,0:T(8,128)S(1)}) custom-call(bf16[150,16384]{1,0:T(8,128)(2,1)} %bitcast.11, s32[2,150]{1,0:T(2,128)S(1)} %bitcast.10, s32[4,250]{1,0:T(4,128)S(1)} %copy-done.4, f32[3,32]{1,0:T(4,128)S(1)} %pad_maximum_fusion.spots), custom_call_target="tpu_custom_call" | custom-call | tf_op jit(solution)/shard_map/exchange/pallas_call | solution.py:232
  136.2 0.0 copy-start.1
  136.2 2.2 %copy-done.1 = bf16[4,4,150,1024]{3,2,1,0:T(8,128)(2,1)} copy-done((bf16[4,4,150,1024]{3,2,1,0:T(8,128)(2,1)}, bf16[4,4,150,1024]{3,2,1,0:T(8,128)(2,1)S(1)}, u32[]{:S(2)}) %copy-start.1) | copy-done | bytes 4915224
  138.4 0.0 copy-start.2
  138.4 0.9 copy-done.2
  139.3 0.0 copy-start.3
  139.3 0.6 copy-done.3
  139.9 16.1 %geometry.1 = (f32[3,320,1024]{2,1,0:T(8,128)}, f32[3,32,1024]{2,1,0:T(8,128)}) custom-call(bf16[4,4,150,1024]{3,2,1,0:T(8,128)(2,1)} %copy-done.1, bf16[4,4,640,150]{3,2,1,0:T(8,128)(2,1)} %get-tuple-element.7.r, f32[4,320,128]{2,1,0:T(8,128)} %copy-done.2, f32[32,320]{1,0:T(8,128)} %copy-done.3, f32[4,3,1024]{2,1,0:T(4,128)} %copy.8.look), custom_call_target="tpu_custom_call" | custom-call | tf_op jit(solution)/shard_map/geometry/pallas_call | solution.py:259
  (2 shorter events, 0.0 us)
Async XLA Ops:
  0.6 2.8 %copy-start = (f32[4,3,16384]{2,0,1:T(4,128)S(1)}, f32[4,3,16384]{2,0,1:T(4,128)}, u32[]{:S(2)}) copy-start(f32[4,3,16384]{2,0,1:T(4,128)} %param.9) | copy-start | bytes 2359300
  4.1 0.7 copy-start.4
  4.8 0.7 copy-start.5
  136.2 2.2 %copy-start.1 = (bf16[4,4,150,1024]{3,2,1,0:T(8,128)(2,1)}, bf16[4,4,150,1024]{3,2,1,0:T(8,128)(2,1)S(1)}, u32[]{:S(2)}) copy-start(bf16[4,4,150,1024]{3,2,1,0:T(8,128)(2,1)S(1)} %get-tuple-element.6.ph) | copy-start | bytes 14745604
  138.4 0.9 copy-start.2
  139.3 0.6 copy-start.3
